TPU v7x, 32 devices: a whole 2x2x4 slice. The times are simulated.
32 devices in a mesh: rep: 4 (over z), own: 8 (over y, x, core).
Axes of the slice: x: 2, y: 2, z: 4, core: 2. Of those that a mesh axis runs over, the one named last changes fastest.
Arguments:
- grads: float32 [16, 576, 1024], P('rep', 'own'), may hold values from -60 to 60
- momentum: bfloat16 [32, 576, 1024], P(('rep', 'own')), may hold values from -6 to 6
- owner_table: int32 [4, 8], replicated, may hold values from 0 to 7, each once within a row
Outputs:
- new_momentum: bfloat16 [32, 576, 1024], P(('rep', 'own'))
- updates: bfloat16 [16, 576, 1024], P(None, 'own')
Inputs may be any that keep to these rules, and one draw needn't show every extreme that they name: Each row of owner_table is a permutation of 0 to 7; entries of 4 or more mark empty slots.
All inputs are finite; a program needn't handle non-finite values.
Results may differ from a plain program's by a relative error of at most 0.01.
Values may be sent and summed in bfloat16 or wider, within the bound.
No kernel may reach another device: no remote copies, remote signals or barrier semaphores. Data moves between devices by JAX's collectives and lax.ppermute only.
A program may use at most 128 MiB of HBM per device.

v0:
```python
import math
import jax
import jax.numpy as jnp
from jax import lax
from jax.sharding import PartitionSpec as P

ITERS = 2
DECAY = 0.95
COEF_A = 3.4445
COEF_B = -4.775
COEF_C = 2.0315
EPSILON = 1e-07


def orthogonalize(blend):
    total = jnp.sqrt(jnp.sum(blend * blend))
    iterate = (blend / (total + EPSILON)).astype(jnp.bfloat16)
    factor = 0.2 * math.sqrt(max(blend.shape[0], blend.shape[1]))
    result = None
    for turn in range(ITERS):
        gram = jnp.dot(iterate, iterate.T, preferred_element_type=jnp.float32).astype(jnp.bfloat16)
        square = jnp.dot(gram, gram, preferred_element_type=jnp.float32)
        poly = (COEF_B * gram.astype(jnp.float32) + COEF_C * square).astype(jnp.bfloat16)
        mixed = COEF_A * iterate.astype(jnp.float32) + jnp.dot(
            poly, iterate, preferred_element_type=jnp.float32
        )
        if turn + 1 < ITERS:
            iterate = mixed.astype(jnp.bfloat16)
        else:
            result = (factor * mixed).astype(jnp.bfloat16)
    return result


def body(grads, momentum, owner_table):
    group = lax.axis_index("rep")
    slot_matrix = lax.dynamic_index_in_dim(owner_table, group, 0, keepdims=False)
    matrix_count, shard_rows, columns = grads.shape
    is_live = slot_matrix < matrix_count
    clamped = jnp.minimum(slot_matrix, matrix_count - 1)
    half_grads = grads.astype(jnp.bfloat16)
    outgoing = jnp.take(half_grads, clamped, axis=0) * is_live[:, None, None].astype(jnp.bfloat16)
    incoming = lax.all_to_all(outgoing, "own", split_axis=0, concat_axis=1, tiled=True)
    gradient = incoming[0].astype(jnp.float32)
    moment = DECAY * momentum[0].astype(jnp.float32) + gradient
    new_momentum = moment.astype(jnp.bfloat16)[None]
    update = orthogonalize(gradient + DECAY * moment)
    returned = lax.all_to_all(update[None], "own", split_axis=1, concat_axis=0, tiled=True)
    holders = jnp.argsort(slot_matrix)[:matrix_count]
    grouped = jnp.take(returned, holders, axis=0)
    updates = lax.all_gather(grouped, "rep", axis=0, tiled=True)
    return (new_momentum, updates)


def solution(mesh):
    in_specs = (P("rep", "own", None), P(("rep", "own"), None, None), P())
    out_specs = (P(("rep", "own"), None, None), P(None, "own", None))
    return jax.shard_map(body, mesh=mesh, in_specs=in_specs, out_specs=out_specs, check_vma=False)
```

profile of v0, /device:TPU:0, one launch (start us, length us, event | category | flops | bytes accessed | tf_op | source)
XLA Modules:
  0.0 138.9 jit_solution(14850939103805925869)
XLA Ops:
  7.2 0.7 compare_convert_fusion
  7.9 0.7 fusion.10
  8.6 1.4 convert_element_type.90
  9.9 0.6 gather_fusion
  10.6 0.2 select_multiply_fusion
  10.8 21.7 %all_to_all.21 = bf16[8,72,1024]{2,1,0:T(8,128)(2,1)S(1)} all-to-all(bf16[8,72,1024]{2,1,0:T(8,128)(2,1)S(1)} %select_multiply_fusion), channel_id=1, replica_groups=mesh['rep'=4,'own'=8] {'own'}, dimensions={0} | all-to-all | bytes 2359296 | tf_op jit(solution)/shard_map/all_to_all | solution.py:42
  32.5 0.3 convert_element_type.111
  32.8 1.0 copy-done
  33.8 1.5 %convert_multiply_fusion = (f32[1,576,1024]{2,1,0:T(8,128)S(1)}, bf16[1,576,1024]{2,1,0:T(8,128)(2,1)}) fusion(bf16[1,576,1024]{2,1,0:T(8,128)(2,1)S(1)} %copy-done, f32[1,576,1024]{2,1,0:T(8,128)S(1)} %bitcast.46), kind=kLoop, calls=%fused_computation.13 | loop fusion | flops 2359296 | bytes 7077888 | tf_op jit(solution)/shard_map/mul | solution.py:44
  35.3 1.2 multiply_reduce_fusion
  37.2 0.5 divide_convert_fusion
  37.7 1.1 convolution_convert_fusion.1
  38.8 0.1 copy-done.1
  39.0 0.6 fusion.4
  39.6 1.7 %add_convert_fusion = bf16[576,1024]{1,0:T(8,128)(2,1)S(1)} fusion(bf16[576,1024]{1,0:T(8,128)(2,1)S(1)} %fusion.4, bf16[576,576]{1,0:T(8,128)(2,1)S(1)} %convolution_convert_fusion.1), kind=kOutput, calls=%fused_computation.9 | convolution fusion | flops 1065701376 | bytes 3022848 | tf_op jit(solution)/shard_map/dot_general | solution.py:24
  41.3 1.1 convolution_convert_fusion
  42.4 1.7 %fusion.5 = bf16[1,576,1024]{2,1,0:T(8,128)(2,1)S(1)} fusion(bf16[576,1024]{1,0:T(8,128)(2,1)S(1)} %add_convert_fusion, bf16[576,576]{1,0:T(8,128)(2,1)S(1)} %convolution_convert_fusion), kind=kOutput, calls=%fused_computation.17 | convolution fusion | flops 1066291200 | bytes 3022848 | tf_op jit(solution)/shard_map/dot_general | solution.py:24
  44.1 1.8 %copy.9 = bf16[1,576,1024]{2,0,1:T(2,128)(2,1)S(1)} copy(bf16[1,576,1024]{2,1,0:T(8,128)(2,1)S(1)} %fusion.5) | data formatting | bytes 2359296 | tf_op jit(solution)/shard_map/broadcast_in_dim | solution.py:47
  46.0 0.5 broadcast.140
  46.5 7.7 %reduce.3 = bf16[576,1024]{1,0:T(8,128)(2,1)S(1)} reduce(bf16[576,1,1024]{2,1,0:T(2,128)(2,1)S(1)} %bitcast.47, bf16[]{:T(256)} %broadcast.140), dimensions={1}, to_apply=%bitcast.43.reduce_sub_computation | reduce | bytes 2359298
  54.2 1.6 %reshape.107 = bf16[8,2,36864]{2,1,0:T(2,128)(2,1)} reshape(bf16[576,1024]{1,0:T(8,128)(2,1)S(1)} %reduce.3) | data formatting | bytes 2359296
  55.8 3.6 %all-to-all-start.1 = ((bf16[8,2,36864]{2,1,0:T(2,128)(2,1)}), bf16[8,2,36864]{2,1,0:T(2,128)(2,1)S(1)}, u32[]{:S(2)}, u32[]{:S(2)}) async-start(bf16[8,2,36864]{2,1,0:T(2,128)(2,1)} %reshape.107), calls=%async_computation.1 | async-start | bytes 2359296 | tf_op jit(solution)/shard_map/all_to_all | solution.py:47
  59.4 0.0 all-gather.2.cloned.1.call-start
  59.4 1.0 sort.17
  60.5 15.6 %all-to-all-done.1 = bf16[8,2,36864]{2,1,0:T(2,128)(2,1)S(1)} async-done(((bf16[8,2,36864]{2,1,0:T(2,128)(2,1)}), bf16[8,2,36864]{2,1,0:T(2,128)(2,1)S(1)}, u32[]{:S(2)}, u32[]{:S(2)}) %all-to-all-start.1) | async-done | bytes 1179680 | tf_op jit(solution)/shard_map/all_to_all | solution.py:47
  76.1 1.1 reshape.108
  77.2 0.4 copy.7
  77.7 0.6 gather_fusion.1
  78.3 0.9 broadcast_select_fusion
  79.2 0.0 all-gather.2.cloned.1.call-update
  79.2 49.5 %all-gather.2.cloned.1.call-done = bf16[16,72,1024]{2,1,0:T(8,128)(2,1)} async-done(((bf16[4,72,1024]{2,1,0:T(8,128)(2,1)}), bf16[16,72,1024]{2,1,0:T(8,128)(2,1)}) %all-gather.2.cloned.1.call-update) | async-done | bytes 2359312 | tf_op jit(solution)/shard_map/all_gather | solution.py:50
  128.8 3.3 %copy.11 = bf16[16,72,1024]{2,1,0:T(8,128)(2,1)} copy(bf16[16,72,1024]{2,1,0:T(8,128)(2,1)} %all-gather.2.cloned.1.call-done) | data formatting | bytes 4718592
  (7 shorter events, 0.0 us)
Async XLA Ops:
  32.5 1.3 copy-start
  37.7 1.3 copy-start.1
  55.8 20.3 %all-to-all-start.1 = ((bf16[8,2,36864]{2,1,0:T(2,128)(2,1)}), bf16[8,2,36864]{2,1,0:T(2,128)(2,1)S(1)}, u32[]{:S(2)}, u32[]{:S(2)}) async-start(bf16[8,2,36864]{2,1,0:T(2,128)(2,1)} %reshape.107), calls=%async_computation.1 | async-start | bytes 2359296 | tf_op jit(solution)/shard_map/all_to_all | solution.py:47
  59.4 69.4 %all-gather.2.cloned.1.call-start = ((), (), s32[]{:S(2)}) async-start(), calls=%async_computation.2 | async-start | bytes 2949120 | tf_op jit(solution)/shard_map/all_gather | solution.py:50
Sparse Core Ops, SparseCore 0:
  79.4 49.3 all-gather.1
where the time goes:
time: 139 us
  waiting for transfers between devices  65.1 us (47%)
  blocking collectives  21.7 us (16%)
  other arithmetic  16.7 us (12%)
  between operations  14.9 us (11%)
  local copies, waits for them, and re-layouts  11.1 us (8%)
  matrix products  5.68 us (4%)
  starting transfers between devices  3.61 us (3%)
    all_gather x1, waiting for transfers between devices, body(): updates = lax.all_gather(grouped, 'rep', axis=0, tiled=True)  49.5 us
    all_to_all x1, blocking collectives, body(): lax.all_to_all(outgoing, 'own', split_axis=0, concat_axis=1, tiled=True)  21.7 us
    all_to_all x1, waiting for transfers between devices, body(): lax.all_to_all(update[None], 'own', split_axis=1, concat_axis=0, tiled=True)  15.6 us
    unnamed x9, local copies, waits for them, and re-layouts  8.11 us
    unnamed x1, other arithmetic  7.72 us
    all_to_all x1, starting transfers between devices, body(): lax.all_to_all(update[None], 'own', split_axis=1, concat_axis=0, tiled=True)  3.56 us
    dot_general x2, matrix products, orthogonalize(): jnp.dot(poly, iterate, preferred_element_type=jnp.float32)  3.45 us
  transfers between devices with their start and end apart: 2, of which 2 were waited for; matrix products, arithmetic and copies ran while one was open for 1% of the time, Pallas kernels for 0%

commit v1 on v0

--- a/solution.py
+++ b/solution.py
@@ -47,7 +47,12 @@
     returned = lax.all_to_all(update[None], "own", split_axis=1, concat_axis=0, tiled=True)
     holders = jnp.argsort(slot_matrix)[:matrix_count]
     grouped = jnp.take(returned, holders, axis=0)
-    updates = lax.all_gather(grouped, "rep", axis=0, tiled=True)
+    ring = [grouped]
+    for hop in range(3):
+        ring.append(lax.ppermute(ring[-1], "rep", [(dev, (dev + 1) % 4) for dev in range(4)]))
+    updates = jnp.roll(
+        jnp.concatenate(ring[::-1], axis=0), (lax.axis_index("rep") + 1) * ring[0].shape[0], axis=0
+    )
     return (new_momentum, updates)
 
 

time: 139 us -> 121 us (0.87)
  waiting for transfers between devices: 65.1 us -> 45.8 us
  blocking collectives: 21.7 us -> 40.9 us
  between operations: 14.9 us -> 1.53 us
  local copies, waits for them, and re-layouts: 11.1 us -> 8.91 us
  starting transfers between devices: 3.61 us -> 1.64 us
    all_gather x1 -> x0, waiting for transfers between devices: 49.5 us -> none  [body(): updates = lax.all_gather(grouped, 'rep', axis=0, tiled=True)]
    ppermute x0 -> x3, waiting for transfers between devices: none -> 45.8 us  [body(): lax.ppermute(ring[-1], 'rep', [(dev, (dev + 1) % 4) for dev in range(4)])]
    all_to_all x0 -> x1, blocking collectives: none -> 19.1 us  [body(): lax.all_to_all(update[None], 'own', split_axis=1, concat_axis=0, tiled=True)]
    all_to_all x1 -> x0, waiting for transfers between devices: 15.6 us -> none  [body(): lax.all_to_all(update[None], 'own', split_axis=1, concat_axis=0, tiled=True)]
    unnamed x9 -> x14, local copies, waits for them, and re-layouts: 8.11 us -> 4.26 us
    all_to_all x1 -> x0, starting transfers between devices: 3.56 us -> none  [body(): lax.all_to_all(update[None], 'own', split_axis=1, concat_axis=0, tiled=True)]
    ppermute x0 -> x3, starting transfers between devices: none -> 1.64 us  [body(): lax.ppermute(ring[-1], 'rep', [(dev, (dev + 1) % 4) for dev in range(4)])]
    dynamic_slice x0 -> x1, local copies, waits for them, and re-layouts: none -> 1.62 us  [body(): jnp.roll(jnp.concatenate(ring[::-1], axis=0), (lax.axis_index('rep') + 1)...]
  transfers between devices with their start and end apart: 2 -> 3, of which waited for: 2 -> 3; matrix products, arithmetic and copies ran while one was open for 1% -> 0% of each run, Pallas kernels for 0% -> 0%
where the time goes in v1:
time: 121 us
  waiting for transfers between devices  45.8 us (38%)
  blocking collectives  40.9 us (34%)
  other arithmetic  16.2 us (13%)
  local copies, waits for them, and re-layouts  8.91 us (7%)
  matrix products  5.68 us (5%)
  starting transfers between devices  1.64 us (1%)
  between operations  1.53 us (1%)
    ppermute x3, waiting for transfers between devices, body(): lax.ppermute(ring[-1], 'rep', [(dev, (dev + 1) % 4) for dev in range(4)])  45.8 us
    all_to_all x1, blocking collectives, body(): lax.all_to_all(outgoing, 'own', split_axis=0, concat_axis=1, tiled=True)  21.7 us
    all_to_all x1, blocking collectives, body(): lax.all_to_all(update[None], 'own', split_axis=1, concat_axis=0, tiled=True)  19.1 us
    unnamed x2, other arithmetic  7.91 us
    unnamed x14, local copies, waits for them, and re-layouts  4.26 us
    dot_general x2, matrix products, orthogonalize(): jnp.dot(poly, iterate, preferred_element_type=jnp.float32)  3.45 us
  transfers between devices with their start and end apart: 3, of which 3 were waited for; matrix products, arithmetic and copies ran while one was open for 0% of the time, Pallas kernels for 0%

profile of v1, /device:TPU:0, one launch (start us, length us, event | category | flops | bytes accessed | tf_op | source)
XLA Modules:
  0.0 120.6 jit_solution(4126468157628201671)
XLA Ops:
  0.6 0.7 fusion.10
  1.3 0.7 compare_convert_fusion
  2.0 1.0 sort.17
  3.0 1.4 %convert_element_type.90 = bf16[4,72,1024]{2,1,0:T(8,128)(2,1)S(1)} convert(f32[4,72,1024]{2,1,0:T(8,128)} %param.3) | non-fusion elementwise | flops 294912 | bytes 1769472 | tf_op jit(solution)/shard_map/convert_element_type | solution.py:40
  4.4 0.6 gather_fusion
  5.0 0.2 select_multiply_fusion
  5.2 21.7 %all_to_all.21 = bf16[8,72,1024]{2,1,0:T(8,128)(2,1)S(1)} all-to-all(bf16[8,72,1024]{2,1,0:T(8,128)(2,1)S(1)} %select_multiply_fusion), channel_id=1, replica_groups=mesh['rep'=4,'own'=8] {'own'}, dimensions={0} | all-to-all | bytes 2359296 | tf_op jit(solution)/shard_map/all_to_all | solution.py:42
  26.9 0.3 convert_element_type.111
  27.2 1.0 copy-done
  28.2 1.5 %convert_multiply_fusion = (f32[1,576,1024]{2,1,0:T(8,128)S(1)}, bf16[1,576,1024]{2,1,0:T(8,128)(2,1)}) fusion(bf16[1,576,1024]{2,1,0:T(8,128)(2,1)S(1)} %copy-done, f32[1,576,1024]{2,1,0:T(8,128)S(1)} %bitcast.46), kind=kLoop, calls=%fused_computation.13 | loop fusion | flops 2359296 | bytes 7077888 | tf_op jit(solution)/shard_map/mul | solution.py:44
  29.7 1.2 %multiply_reduce_fusion = f32[]{:T(128)} fusion(f32[8,72,1024]{2,1,0:T(8,128)S(1)} %bitcast.44, bf16[8,72,1024]{2,1,0:T(8,128)(2,1)S(1)} %all_to_all.21), kind=kLoop, calls=%fused_computation.11 | loop fusion | flops 3538943 | bytes 3538948 | tf_op jit(solution)/shard_map/reduce_sum | solution.py:16
  31.6 0.5 divide_convert_fusion
  32.1 1.1 convolution_convert_fusion.1
  33.4 0.6 fusion.4
  34.0 1.7 %add_convert_fusion = bf16[576,1024]{1,0:T(8,128)(2,1)S(1)} fusion(bf16[576,1024]{1,0:T(8,128)(2,1)S(1)} %fusion.4, bf16[576,576]{1,0:T(8,128)(2,1)S(1)} %convolution_convert_fusion.1), kind=kOutput, calls=%fused_computation.9 | convolution fusion | flops 1065701376 | bytes 3022848 | tf_op jit(solution)/shard_map/dot_general | solution.py:24
  35.7 1.1 convolution_convert_fusion
  36.8 1.7 %fusion.5 = bf16[1,576,1024]{2,1,0:T(8,128)(2,1)S(1)} fusion(bf16[576,1024]{1,0:T(8,128)(2,1)S(1)} %add_convert_fusion, bf16[576,576]{1,0:T(8,128)(2,1)S(1)} %convolution_convert_fusion), kind=kOutput, calls=%fused_computation.17 | convolution fusion | flops 1066291200 | bytes 3022848 | tf_op jit(solution)/shard_map/dot_general | solution.py:24
  38.6 1.8 %copy.9 = bf16[1,576,1024]{2,0,1:T(2,128)(2,1)S(1)} copy(bf16[1,576,1024]{2,1,0:T(8,128)(2,1)S(1)} %fusion.5) | data formatting | bytes 2359296 | tf_op jit(solution)/shard_map/broadcast_in_dim | solution.py:47
  40.4 0.5 broadcast.141
  40.9 7.7 %reduce.3 = bf16[576,1024]{1,0:T(8,128)(2,1)S(1)} reduce(bf16[576,1,1024]{2,1,0:T(2,128)(2,1)S(1)} %bitcast.47, bf16[]{:T(256)} %broadcast.141), dimensions={1}, to_apply=%bitcast.43.reduce_sub_computation | reduce | bytes 2359298
  48.7 0.8 reshape.107
  49.5 19.1 %all_to_all.22 = bf16[8,2,36864]{2,1,0:T(2,128)(2,1)S(1)} all-to-all(bf16[8,2,36864]{2,1,0:T(2,128)(2,1)S(1)} %reshape.107), channel_id=1, replica_groups=mesh['rep'=4,'own'=8] {'own'}, dimensions={0} | all-to-all | bytes 2359296 | tf_op jit(solution)/shard_map/all_to_all | solution.py:47
  68.6 1.1 reshape.108
  69.7 0.4 copy.7
  70.2 0.6 gather_fusion.1
  70.9 1.6 %collective-permute-start = (bf16[4,72,1024]{2,1,0:T(8,128)(2,1)S(1)}, bf16[4,72,1024]{2,1,0:T(8,128)(2,1)S(1)}, u32[]{:S(2)}, u32[]{:S(2)}) collective-permute-start(bf16[4,72,1024]{2,1,0:T(8,128)(2,1)S(1)} %broadcast_select_fusion), channel_id=1, source_target_pairs={{0,8},{8,16},{16,24},{24,0},{1,9},{9,17},{17,25},{25,1},{2,10},{10... | collective-permute-start | bytes 1769480 | tf_op jit(solution)/shard_map/ppermute | solution.py:52
  72.5 15.1 %collective-permute-done = bf16[4,72,1024]{2,1,0:T(8,128)(2,1)S(1)} collective-permute-done((bf16[4,72,1024]{2,1,0:T(8,128)(2,1)S(1)}, bf16[4,72,1024]{2,1,0:T(8,128)(2,1)S(1)}, u32[]{:S(2)}, u32[]{:S(2)}) %collective-permute-start) | collective-permute-done | bytes 589856 | tf_op jit(solution)/shard_map/ppermute | solution.py:52
  87.6 15.8 %collective-permute-done.1 = bf16[4,72,1024]{2,1,0:T(8,128)(2,1)S(1)} collective-permute-done((bf16[4,72,1024]{2,1,0:T(8,128)(2,1)S(1)}, bf16[4,72,1024]{2,1,0:T(8,128)(2,1)S(1)}, u32[]{:S(2)}, u32[]{:S(2)}) %collective-permute-start.1) | collective-permute-done | bytes 589856 | tf_op jit(solution)/shard_map/ppermute | solution.py:52
  103.4 14.9 %collective-permute-done.2 = bf16[4,72,1024]{2,1,0:T(8,128)(2,1)S(1)} collective-permute-done((bf16[4,72,1024]{2,1,0:T(8,128)(2,1)S(1)}, bf16[4,72,1024]{2,1,0:T(8,128)(2,1)S(1)}, u32[]{:S(2)}, u32[]{:S(2)}) %collective-permute-start.2) | collective-permute-done | bytes 589856 | tf_op jit(solution)/shard_map/ppermute | solution.py:52
  118.4 0.2 constant_dynamic-update-slice_fusion.4
  118.8 0.2 constant_dynamic-update-slice_fusion
  119.0 1.6 %constant_dynamic-slice_fusion = bf16[16,72,1024]{2,1,0:T(8,128)(2,1)} fusion(bf16[32,72,1024]{2,1,0:T(8,128)(2,1)S(1)} %constant_dynamic-update-slice_fusion, s32[]{:T(128)S(6)} %select_n.53), kind=kLoop, calls=%fused_computation.43 | loop fusion | bytes 4718596 | tf_op jit(solution)/shard_map/jit(_roll_dynamic)/dynamic_slice | solution.py:53
  (16 shorter events, 0.5 us)
Async XLA Ops:
  26.9 1.3 %copy-start = (bf16[1,576,1024]{2,1,0:T(8,128)(2,1)S(1)}, bf16[1,576,1024]{2,1,0:T(8,128)(2,1)}, u32[]{:S(2)}) copy-start(bf16[1,576,1024]{2,1,0:T(8,128)(2,1)} %param.4) | copy-start | bytes 3538948
  32.1 1.3 %copy-start.1 = (bf16[1,576,1024]{2,1,0:T(8,128)(2,1)S(1)}, bf16[1,576,1024]{2,1,0:T(8,128)(2,1)}, u32[]{:S(2)}) copy-start(bf16[1,576,1024]{2,1,0:T(8,128)(2,1)} %param.4) | copy-start | bytes 3538948
  70.9 16.7 %collective-permute-start = (bf16[4,72,1024]{2,1,0:T(8,128)(2,1)S(1)}, bf16[4,72,1024]{2,1,0:T(8,128)(2,1)S(1)}, u32[]{:S(2)}, u32[]{:S(2)}) collective-permute-start(bf16[4,72,1024]{2,1,0:T(8,128)(2,1)S(1)} %broadcast_select_fusion), channel_id=1, source_target_pairs={{0,8},{8,16},{16,24},{24,0},{1,9},{9,17},{17,25},{25,1},{2,10},{10... | collective-permute-start | bytes 1769480 | tf_op jit(solution)/shard_map/ppermute | solution.py:52
  87.6 15.8 %collective-permute-start.1 = (bf16[4,72,1024]{2,1,0:T(8,128)(2,1)S(1)}, bf16[4,72,1024]{2,1,0:T(8,128)(2,1)S(1)}, u32[]{:S(2)}, u32[]{:S(2)}) collective-permute-start(bf16[4,72,1024]{2,1,0:T(8,128)(2,1)S(1)} %collective-permute-done), channel_id=1, source_target_pairs={{0,8},{8,16},{16,24},{24,0},{1,9},{9,17},{17,25},{25,1},{2,10},{10... | collective-permute-start | bytes 1769480 | tf_op jit(solution)/shard_map/ppermute | solution.py:52
  103.4 14.9 %collective-permute-start.2 = (bf16[4,72,1024]{2,1,0:T(8,128)(2,1)S(1)}, bf16[4,72,1024]{2,1,0:T(8,128)(2,1)S(1)}, u32[]{:S(2)}, u32[]{:S(2)}) collective-permute-start(bf16[4,72,1024]{2,1,0:T(8,128)(2,1)S(1)} %collective-permute-done.1), channel_id=1, source_target_pairs={{0,8},{8,16},{16,24},{24,0},{1,9},{9,17},{17,25},{25,1},{2,10},{10... | collective-permute-start | bytes 1769480 | tf_op jit(solution)/shard_map/ppermute | solution.py:52
